TPU v7x, 32 devices: a whole 2x2x4 slice. The times are simulated.
32 devices in a mesh: cluster: 8 (over z, y), sub: 4 (over x, core).
Axes of the slice: x: 2, y: 2, z: 4, core: 2. Of those that a mesh axis runs over, the one named last changes fastest.
Arguments:
- rhs: float32 [128, 4, 384], P(('cluster', 'sub')), may hold values from -8 to 8
- operators: bfloat16 [128, 384, 384], P(('cluster', 'sub')), may hold values from -1 to 5
- signs: int32 [128, 384], P(('cluster', 'sub')), may hold values from -1 to 1, as said below
- links: int32 [128, 3, 128], P(('cluster', 'sub')), may hold values from 0 to 127, as said below
- cluster_basis: float32 [128, 24, 384], P(('cluster', 'sub')), may hold values from -0.3125 to 0.3125
- corner_basis: float32 [128, 8, 384], P(('cluster', 'sub')), may hold values from -0.3125 to 0.3125
- corner_ids: int32 [128, 8], P(('cluster', 'sub')), may hold values from 0 to 127
- cluster_coarse: float32 [8, 384, 384], P('cluster', 'sub'), may hold values from -1 to 3
- global_coarse: float32 [128, 128], P('sub'), may hold values from -0.2 to 0.5
Outputs:
- multipliers: float32 [128, 4, 384], P(('cluster', 'sub'))
- residual: float32 [128, 4, 384], P(('cluster', 'sub'))
Inputs may be any that keep to these rules, and one draw needn't show every extreme that they name: `signs`: each entry is -1 or 1. Each links[s, b] is a permutation of 0 to 127; both subdomains of an interface pair hold the same permutation for it.
All inputs are finite; a program needn't handle non-finite values.
Results may differ from a plain program's by a relative error of at most 0.007.
Values sent between devices are 32-bit elements; how exact they have to be, the bound alone decides.
A program may use at most 64 MiB of HBM per device.

v0:
```python
import jax
import jax.numpy as jnp
from jax import lax
from jax.sharding import PartitionSpec as P

ITERS = 2


HIGHEST_PRECISION = lax.Precision.HIGHEST


def extended(block, sides, width):
    for axis, dim in sides:
        count = lax.axis_size(axis)
        forward = [(i, i + 1) for i in range(count - 1)]
        backward = [(target, source) for source, target in forward]
        low = lax.ppermute(
            lax.slice_in_dim(block, block.shape[dim] - width, None, axis=dim), axis, forward
        )
        high = lax.ppermute(lax.slice_in_dim(block, 0, width, axis=dim), axis, backward)
        block = jnp.concatenate([low, block, high], axis=dim)
    return block


def invert(order):
    row_index = jnp.broadcast_to(jnp.arange(order.shape[0], dtype=jnp.int32)[:, None], order.shape)
    col_index = jnp.broadcast_to(jnp.arange(order.shape[1], dtype=jnp.int32)[None, :], order.shape)
    return jnp.zeros_like(order).at[row_index, order].set(col_index)


def permuted(blocks, order):
    return jnp.take_along_axis(blocks, order[:, None, :], axis=2)


def interface(vector, tables):
    inv_up, order_down, inv_even, order_odd = tables
    block_width = vector.shape[2] // 3
    up_part = vector[:, :, :block_width]
    down_part = vector[:, :, block_width : 2 * block_width]
    across = vector[:, :, 2 * block_width :]
    send_up = permuted(up_part, inv_up)
    send_down = permuted(down_part, order_down)
    inside_rims = extended(jnp.stack([send_down, send_up]), (("sub", 0),), 1)
    send_even = permuted(across[0::2], inv_even)
    send_odd = permuted(across[1::2], order_odd)
    outside_rims = extended(jnp.stack([send_odd, send_even]), (("cluster", 0),), 1)
    new_across = jnp.stack([outside_rims[3], outside_rims[0]], axis=1).reshape(across.shape)
    return jnp.concatenate([inside_rims[3], inside_rims[0], new_across], axis=2)


def apply(vector, sign_field, operators, tables):
    spread = sign_field * (vector + interface(vector, tables))
    product = jnp.einsum(
        "srk,skl->srl", spread.astype(jnp.bfloat16), operators, preferred_element_type=jnp.float32
    )
    curvature = lax.psum(jnp.sum(spread * product, axis=(0, 2)), ("cluster", "sub"))
    signed = sign_field * product
    result = signed + interface(signed, tables)
    return (result, curvature)


def project(vector, coarse):
    cluster_basis, corner_basis, flat_ids, onehot, cluster_coarse, global_coarse = coarse
    load_count = vector.shape[1]
    local_subs = vector.shape[0]
    cluster_coef = jnp.einsum("srl,skl->srk", vector, cluster_basis, precision=HIGHEST_PRECISION)
    own_coef = cluster_coef.transpose(1, 0, 2).reshape(load_count, -1)
    part_cluster = jnp.dot(own_coef, cluster_coarse[0], precision=HIGHEST_PRECISION)
    corner_coef = jnp.einsum(
        "scl,srl->rsc", corner_basis, vector, precision=HIGHEST_PRECISION
    ).reshape(load_count, -1)
    corner_local = jnp.dot(corner_coef, onehot, precision=HIGHEST_PRECISION)
    squares = jnp.sum(vector * vector, axis=(0, 2))
    row_count = global_coarse.shape[0]
    corner_whole, total_norm = lax.psum((corner_local, squares), ("cluster", "sub"))
    corner_rows = lax.dynamic_slice_in_dim(
        corner_whole, lax.axis_index("sub") * row_count, row_count, 1
    )
    part_global = jnp.dot(corner_rows, global_coarse, precision=HIGHEST_PRECISION)
    cluster_all, global_all = lax.psum((part_cluster, part_global), "sub")
    own_width = own_coef.shape[1]
    cluster_own = lax.dynamic_slice_in_dim(
        cluster_all, lax.axis_index("sub") * own_width, own_width, 1
    )
    cluster_own = cluster_own.reshape(load_count, local_subs, -1)
    fix_cluster = jnp.einsum(
        "rsk,skl->srl", cluster_own, cluster_basis, precision=HIGHEST_PRECISION
    )
    picked = jnp.take(global_all, flat_ids, axis=1).reshape(load_count, local_subs, -1)
    fix_corner = jnp.einsum("rsc,scl->srl", picked, corner_basis, precision=HIGHEST_PRECISION)
    return (vector - fix_cluster - fix_corner, total_norm)


def local(
    rhs,
    operators,
    signs,
    links,
    cluster_basis,
    corner_basis,
    corner_ids,
    cluster_coarse,
    global_coarse,
):
    sign_field = signs.astype(jnp.float32)[:, None, :]
    tables = (invert(links[:, 0]), links[:, 1], invert(links[0::2, 2]), links[1::2, 2])
    flat_ids = corner_ids.reshape(-1)
    onehot = (
        flat_ids[:, None] == jnp.arange(global_coarse.shape[1], dtype=jnp.int32)[None, :]
    ).astype(jnp.float32)
    coarse = (cluster_basis, corner_basis, flat_ids, onehot, cluster_coarse, global_coarse)
    residual = rhs
    projected, residual_norm = project(residual, coarse)
    direction = projected
    multipliers = jnp.zeros_like(rhs)
    for iteration in range(ITERS):
        product, curvature = apply(direction, sign_field, operators, tables)
        step_size = (residual_norm / curvature)[None, :, None]
        multipliers = multipliers + step_size * direction
        residual = residual - step_size * product
        if iteration + 1 < ITERS:
            projected, norm_next = project(residual, coarse)
            direction = projected + (norm_next / residual_norm)[None, :, None] * direction
            residual_norm = norm_next
    return (multipliers, residual)


def solution(mesh):
    placed = (
        P(("cluster", "sub"), None, None),
        P(("cluster", "sub"), None, None),
        P(("cluster", "sub"), None),
        P(("cluster", "sub"), None, None),
        P(("cluster", "sub"), None, None),
        P(("cluster", "sub"), None, None),
        P(("cluster", "sub"), None),
        P("cluster", "sub", None),
        P("sub", None),
    )
    return jax.shard_map(
        local,
        mesh=mesh,
        in_specs=placed,
        out_specs=(P(("cluster", "sub"), None, None), P(("cluster", "sub"), None, None)),
        check_vma=False,
    )
```

profile of v0, /device:TPU:0, one launch (start us, length us, event | category | flops | bytes accessed | tf_op | source)
XLA Modules:
  0.0 321.5 jit_solution(7329631267407565892)
XLA Ops:
  0.7 0.9 eq.15
  2.3 1.2 convolution_bitcast_fusion.3
  3.6 1.0 convolution_bitcast_fusion.2
  4.9 41.9 %psum.72 = f32[4,128]{1,0:T(4,128)S(1)} all-reduce(f32[4,128]{1,0:T(4,128)S(1)} %fusion.16), channel_id=1, replica_groups=mesh['cluster'=8,'sub'=4] {'cluster','sub'}, use_global_device_ids=true, to_apply=%region_3.0 | all-reduce | flops 512 | bytes 4096 | tf_op jit(solution)/shard_map/psum | solution.py:75
  46.8 1.1 fusion.3
  48.0 0.9 fusion.46
  48.9 5.9 %all-reduce.3 = (f32[4,384]{1,0:T(4,128)S(1)}, f32[4,128]{1,0:T(4,128)S(1)}) all-reduce(f32[4,384]{1,0:T(4,128)S(1)} %fusion.3, f32[4,128]{1,0:T(4,128)S(1)} %fusion.46), channel_id=1, replica_groups=mesh['cluster'=8,'sub'=4] {'sub'}, use_global_device_ids=true, to_apply=%region_2.0 | all-reduce | flops 2048 | bytes 16384 | tf_op jit(solution)/shard_map/psum | solution.py:80
  54.9 1.1 convolution_subtract_fusion.3
  56.7 1.1 convolution_subtract_fusion.2
  58.0 1.9 gather_fusion.3
  60.0 1.3 collective-permute-start.2
  61.4 11.4 %scatter_fusion.1 = s32[2,128]{1,0:T(2,128)S(1)} fusion(s32[2,128]{1,0:T(2,128)S(1)} %broadcast.105, s32[256]{0:T(256)S(1)} %fusion.53, s32[256]{0:T(256)S(1)} %iota_bitcast_fusion.1), kind=kCustom, calls=%fused_computation.19 | custom fusion | bytes 5120 | tf_op jit(solution)/shard_map/scatter | solution.py:28
  73.0 1.9 gather_fusion.4
  75.0 5.0 %collective-permute-start.3 = (f32[1,2,4,128]{3,2,1,0:T(4,128)S(1)}, f32[1,2,4,128]{3,2,1,0:T(4,128)S(1)}, u32[]{:S(2)}, u32[]{:S(2)}) collective-permute-start(f32[1,2,4,128]{3,2,1,0:T(4,128)S(1)} %select_bitcast_fusion.6), channel_id=1, source_target_pairs={{0,4},{4,8},{8,12},{12,16},{16,20},{20,24},{24,28},{1,5},{5,9},{9,... | collective-permute-start | bytes 12296 | tf_op jit(solution)/shard_map/ppermute | solution.py:17
  80.2 3.7 %gather_fusion.1 = f32[512,4]{1,0:T(8,128)S(1)} fusion(f32[4,4,128]{1,2,0:T(8,128)S(1)} %copy.49, s32[512]{0:T(512)S(1)} %get-tuple-element.39), kind=kCustom, calls=%fused_computation.1.clone | custom fusion | bytes 20480 | tf_op jit(solution)/shard_map/jit(take_along_axis)/gather | solution.py:32
  84.0 1.3 collective-permute-start
  85.3 22.5 %scatter_fusion = s32[4,128]{1,0:T(4,128)S(1)} fusion(s32[4,128]{1,0:T(4,128)S(1)} %broadcast.103, s32[512]{0:T(512)S(1)} %get-tuple-element.40, s32[512]{0:T(512)S(1)} %iota_bitcast_fusion), kind=kCustom, calls=%fused_computation.18 | custom fusion | bytes 10240 | tf_op jit(solution)/shard_map/scatter | solution.py:28
  108.1 3.7 %gather_fusion.2 = f32[512,4]{1,0:T(8,128)S(1)} fusion(f32[4,4,128]{1,2,0:T(8,128)S(1)} %copy.51, s32[512]{0:T(512)S(1)} %fusion.40), kind=kCustom, calls=%fused_computation.4.clone | custom fusion | bytes 20480 | tf_op jit(solution)/shard_map/jit(take_along_axis)/gather | solution.py:32
  111.9 3.0 collective-permute-start.1
  116.3 1.9 gather_fusion.7
  118.3 1.3 collective-permute-start.6
  119.7 1.9 gather_fusion.8
  121.7 5.8 %collective-permute-start.7 = (f32[1,2,4,128]{3,2,1,0:T(4,128)S(1)}, f32[1,2,4,128]{3,2,1,0:T(4,128)S(1)}, u32[]{:S(2)}, u32[]{:S(2)}) collective-permute-start(f32[1,2,4,128]{3,2,1,0:T(4,128)S(1)} %select_bitcast_fusion.4), channel_id=1, source_target_pairs={{0,4},{4,8},{8,12},{12,16},{16,20},{20,24},{24,28},{1,5},{5,9},{9,... | collective-permute-start | bytes 12296 | tf_op jit(solution)/shard_map/ppermute | solution.py:17
  127.7 3.7 %gather_fusion.5 = f32[512,4]{1,0:T(8,128)S(1)} fusion(f32[4,4,128]{1,2,0:T(8,128)S(1)} %copy.57, s32[512]{0:T(512)S(1)} %get-tuple-element.39), kind=kCustom, calls=%fused_computation.5.clone | custom fusion | bytes 20480 | tf_op jit(solution)/shard_map/jit(take_along_axis)/gather | solution.py:32
  131.4 1.3 collective-permute-start.4
  132.9 3.7 %gather_fusion.6 = f32[512,4]{1,0:T(8,128)S(1)} fusion(f32[4,4,128]{1,2,0:T(8,128)S(1)} %copy.59, s32[512]{0:T(512)S(1)} %fusion.40), kind=kCustom, calls=%fused_computation.6.clone | custom fusion | bytes 20480 | tf_op jit(solution)/shard_map/jit(take_along_axis)/gather | solution.py:32
  136.7 3.0 collective-permute-start.5
  139.7 42.4 %all-reduce.1 = (f32[4]{0:T(128)S(1)}, f32[4]{0:T(128)S(1)}) all-reduce(f32[4]{0:T(128)S(1)} %multiply_reduce_fusion.3, f32[4]{0:T(128)S(1)} %get-tuple-element.17), channel_id=1, replica_groups=mesh['cluster'=8,'sub'=4] {'cluster','sub'}, use_global_device_ids=true, to_apply=%region_1.0 | all-reduce | flops 8 | bytes 64 | tf_op jit(solution)/shard_map/psum | solution.py:75
  183.1 38.6 %all-reduce = (f32[4,128]{1,0:T(4,128)S(1)}, f32[4]{0:T(128)S(1)}) all-reduce(f32[4,128]{1,0:T(4,128)S(1)} %fusion.15, f32[4]{0:T(128)S(1)} %get-tuple-element.13), channel_id=1, replica_groups=mesh['cluster'=8,'sub'=4] {'cluster','sub'}, use_global_device_ids=true, to_apply=%region_12.16 | all-reduce | flops 516 | bytes 4128 | tf_op jit(solution)/shard_map/psum | solution.py:75
  222.2 7.0 %all-reduce.2 = (f32[4,384]{1,0:T(4,128)S(1)}, f32[4,128]{1,0:T(4,128)S(1)}) all-reduce(f32[4,384]{1,0:T(4,128)S(1)} %fusion.1, f32[4,128]{1,0:T(4,128)S(1)} %fusion.44), channel_id=1, replica_groups=mesh['cluster'=8,'sub'=4] {'sub'}, use_global_device_ids=true, to_apply=%region_11.15 | all-reduce | flops 2048 | bytes 16384 | tf_op jit(solution)/shard_map/psum | solution.py:80
  230.9 1.9 gather_fusion.12
  232.9 1.3 collective-permute-start.10
  234.3 1.9 gather_fusion.13
  236.3 4.5 %collective-permute-start.11 = (f32[1,2,4,128]{3,2,1,0:T(4,128)S(1)}, f32[1,2,4,128]{3,2,1,0:T(4,128)S(1)}, u32[]{:S(2)}, u32[]{:S(2)}) collective-permute-start(f32[1,2,4,128]{3,2,1,0:T(4,128)S(1)} %select_bitcast_fusion.2), channel_id=1, source_target_pairs={{0,4},{4,8},{8,12},{12,16},{16,20},{20,24},{24,28},{1,5},{5,9},{9,... | collective-permute-start | bytes 12296 | tf_op jit(solution)/shard_map/ppermute | solution.py:17
  241.0 3.7 %gather_fusion.10 = f32[512,4]{1,0:T(8,128)S(1)} fusion(f32[4,4,128]{1,2,0:T(8,128)S(1)} %copy.71, s32[512]{0:T(512)S(1)} %get-tuple-element.39), kind=kCustom, calls=%fused_computation.7.clone | custom fusion | bytes 20480 | tf_op jit(solution)/shard_map/jit(take_along_axis)/gather | solution.py:32
  244.8 1.3 collective-permute-start.8
  246.3 3.7 %gather_fusion.11 = f32[512,4]{1,0:T(8,128)S(1)} fusion(f32[4,4,128]{1,2,0:T(8,128)S(1)} %copy.73, s32[512]{0:T(512)S(1)} %fusion.40), kind=kCustom, calls=%fused_computation.8.clone | custom fusion | bytes 20480 | tf_op jit(solution)/shard_map/jit(take_along_axis)/gather | solution.py:32
  250.0 3.0 collective-permute-start.9
  253.1 0.8 collective-permute-done.9
  254.3 42.8 %psum.79 = f32[4]{0:T(128)S(1)} all-reduce(f32[4]{0:T(128)S(1)} %get-tuple-element.16), channel_id=1, replica_groups=mesh['cluster'=8,'sub'=4] {'cluster','sub'}, use_global_device_ids=true, to_apply=%region_15.19 | all-reduce | flops 4 | bytes 32 | tf_op jit(solution)/shard_map/psum | solution.py:56
  297.3 1.9 gather_fusion.16
  299.3 1.5 collective-permute-start.14
  300.9 1.9 gather_fusion.17
  302.9 4.8 %collective-permute-start.15 = (f32[1,2,4,128]{3,2,1,0:T(4,128)S(1)}, f32[1,2,4,128]{3,2,1,0:T(4,128)S(1)}, u32[]{:S(2)}, u32[]{:S(2)}) collective-permute-start(f32[1,2,4,128]{3,2,1,0:T(4,128)S(1)} %select_bitcast_fusion), channel_id=1, source_target_pairs={{0,4},{4,8},{8,12},{12,16},{16,20},{20,24},{24,28},{1,5},{5,9},{9,... | collective-permute-start | bytes 12296 | tf_op jit(solution)/shard_map/ppermute | solution.py:17
  307.9 3.7 %gather_fusion.14 = f32[512,4]{1,0:T(8,128)S(1)} fusion(f32[4,4,128]{1,2,0:T(8,128)S(1)} %copy.79, s32[512]{0:T(512)S(1)} %get-tuple-element.39), kind=kCustom, calls=%fused_computation.9.clone | custom fusion | bytes 20480 | tf_op jit(solution)/shard_map/jit(take_along_axis)/gather | solution.py:32
  311.7 1.3 collective-permute-start.12
  313.1 3.7 %gather_fusion.15 = f32[512,4]{1,0:T(8,128)S(1)} fusion(f32[4,4,128]{1,2,0:T(8,128)S(1)} %copy.81, s32[512]{0:T(512)S(1)} %fusion.40), kind=kCustom, calls=%fused_computation.10.clone | custom fusion | bytes 20480 | tf_op jit(solution)/shard_map/jit(take_along_axis)/gather | solution.py:32
  316.9 3.0 collective-permute-start.13
  (142 shorter events, 11.9 us)
Async XLA Ops:
  0.6 115.1 %copy-start = (bf16[4,384,384]{2,1,0:T(8,128)(2,1)S(1)}, bf16[4,384,384]{2,1,0:T(8,128)(2,1)}, u32[]{:S(2)}) copy-start(bf16[4,384,384]{2,1,0:T(8,128)(2,1)} %param.16) | copy-start | bytes 3538948
  0.6 60.7 %copy-start.6 = (s32[4,3,128]{2,0,1:T(4,128)S(1)}, s32[4,3,128]{2,0,1:T(4,128)}, u32[]{:S(2)}) copy-start(s32[4,3,128]{2,0,1:T(4,128)} %param.18) | copy-start | bytes 18436
  60.0 55.0 %collective-permute-start.2 = (f32[1,2,4,128]{3,2,1,0:T(4,128)S(1)}, f32[1,2,4,128]{3,2,1,0:T(4,128)S(1)}, u32[]{:S(2)}, u32[]{:S(2)}) collective-permute-start(f32[1,2,4,128]{3,2,1,0:T(4,128)S(1)} %select_bitcast_fusion.7), channel_id=1, source_target_pairs={{4,0},{8,4},{12,8},{16,12},{20,16},{24,20},{28,24},{5,1},{9,5},{13... | collective-permute-start | bytes 12296 | tf_op jit(solution)/shard_map/ppermute | solution.py:20
  75.0 40.1 %collective-permute-start.3 = (f32[1,2,4,128]{3,2,1,0:T(4,128)S(1)}, f32[1,2,4,128]{3,2,1,0:T(4,128)S(1)}, u32[]{:S(2)}, u32[]{:S(2)}) collective-permute-start(f32[1,2,4,128]{3,2,1,0:T(4,128)S(1)} %select_bitcast_fusion.6), channel_id=1, source_target_pairs={{0,4},{4,8},{8,12},{12,16},{16,20},{20,24},{24,28},{1,5},{5,9},{9,... | collective-permute-start | bytes 12296 | tf_op jit(solution)/shard_map/ppermute | solution.py:17
  84.0 31.1 %collective-permute-start = (f32[1,4,4,128]{3,2,1,0:T(4,128)S(1)}, f32[1,4,4,128]{3,2,1,0:T(4,128)S(1)}, u32[]{:S(2)}, u32[]{:S(2)}) collective-permute-start(f32[1,4,4,128]{3,2,1,0:T(4,128)S(1)} %fusion.28), channel_id=1, source_target_pairs={{1,0},{2,1},{3,2},{5,4},{6,5},{7,6},{9,8},{10,9},{11,10},{13,12},{... | collective-permute-start | bytes 24584 | tf_op jit(solution)/shard_map/ppermute | solution.py:20
  85.3 29.6 %copy-start.3 = (f32[4,4,384]{2,1,0:T(4,128)S(1)}, f32[4,4,384]{2,1,0:T(4,128)}, u32[]{:S(2)}) copy-start(f32[4,4,384]{2,1,0:T(4,128)} %param.15) | copy-start | bytes 73732
  85.3 29.7 %copy-start.7 = (s32[4,384]{1,0:T(4,128)S(1)}, s32[4,384]{1,0:T(4,128)}, u32[]{:S(2)}) copy-start(s32[4,384]{1,0:T(4,128)} %param.17) | copy-start | bytes 18436
  111.9 3.9 %collective-permute-start.1 = (f32[1,4,4,128]{3,2,1,0:T(4,128)S(1)}, f32[1,4,4,128]{3,2,1,0:T(4,128)S(1)}, u32[]{:S(2)}, u32[]{:S(2)}) collective-permute-start(f32[1,4,4,128]{3,2,1,0:T(4,128)S(1)} %fusion.27), channel_id=1, source_target_pairs={{0,1},{1,2},{2,3},{4,5},{5,6},{6,7},{8,9},{9,10},{10,11},{12,13},{... | collective-permute-start | bytes 24584 | tf_op jit(solution)/shard_map/ppermute | solution.py:17
  118.3 63.9 %collective-permute-start.6 = (f32[1,2,4,128]{3,2,1,0:T(4,128)S(1)}, f32[1,2,4,128]{3,2,1,0:T(4,128)S(1)}, u32[]{:S(2)}, u32[]{:S(2)}) collective-permute-start(f32[1,2,4,128]{3,2,1,0:T(4,128)S(1)} %select_bitcast_fusion.5), channel_id=1, source_target_pairs={{4,0},{8,4},{12,8},{16,12},{20,16},{24,20},{28,24},{5,1},{9,5},{13... | collective-permute-start | bytes 12296 | tf_op jit(solution)/shard_map/ppermute | solution.py:20
  119.6 62.8 %copy-start.2 = (f32[4,8,384]{2,1,0:T(8,128)S(1)}, f32[4,8,384]{2,1,0:T(8,128)}, u32[]{:S(2)}) copy-start(f32[4,8,384]{2,1,0:T(8,128)} %param.20) | copy-start | bytes 147460
  119.7 62.8 %copy-start.1 = (f32[4,24,384]{2,1,0:T(8,128)S(1)}, f32[4,24,384]{2,1,0:T(8,128)}, u32[]{:S(2)}) copy-start(f32[4,24,384]{2,1,0:T(8,128)} %param.19) | copy-start | bytes 442372
  121.7 100.0 %copy-start.5 = (f32[32,128]{1,0:T(8,128)S(1)}, f32[32,128]{1,0:T(8,128)}, u32[]{:S(2)}) copy-start(f32[32,128]{1,0:T(8,128)} %param.23) | copy-start | bytes 49156
  121.7 100.3 %copy-start.4 = (f32[1,96,384]{2,1,0:T(8,128)S(1)}, f32[1,96,384]{2,1,0:T(8,128)}, u32[]{:S(2)}) copy-start(f32[1,96,384]{2,1,0:T(8,128)} %param.22) | copy-start | bytes 442372
  121.7 60.4 %collective-permute-start.7 = (f32[1,2,4,128]{3,2,1,0:T(4,128)S(1)}, f32[1,2,4,128]{3,2,1,0:T(4,128)S(1)}, u32[]{:S(2)}, u32[]{:S(2)}) collective-permute-start(f32[1,2,4,128]{3,2,1,0:T(4,128)S(1)} %select_bitcast_fusion.4), channel_id=1, source_target_pairs={{0,4},{4,8},{8,12},{12,16},{16,20},{20,24},{24,28},{1,5},{5,9},{9,... | collective-permute-start | bytes 12296 | tf_op jit(solution)/shard_map/ppermute | solution.py:17
  131.4 50.7 %collective-permute-start.4 = (f32[1,4,4,128]{3,2,1,0:T(4,128)S(1)}, f32[1,4,4,128]{3,2,1,0:T(4,128)S(1)}, u32[]{:S(2)}, u32[]{:S(2)}) collective-permute-start(f32[1,4,4,128]{3,2,1,0:T(4,128)S(1)} %fusion.26), channel_id=1, source_target_pairs={{1,0},{2,1},{3,2},{5,4},{6,5},{7,6},{9,8},{10,9},{11,10},{13,12},{... | collective-permute-start | bytes 24584 | tf_op jit(solution)/shard_map/ppermute | solution.py:20
  136.7 45.5 %collective-permute-start.5 = (f32[1,4,4,128]{3,2,1,0:T(4,128)S(1)}, f32[1,4,4,128]{3,2,1,0:T(4,128)S(1)}, u32[]{:S(2)}, u32[]{:S(2)}) collective-permute-start(f32[1,4,4,128]{3,2,1,0:T(4,128)S(1)} %fusion.25), channel_id=1, source_target_pairs={{0,1},{1,2},{2,3},{4,5},{5,6},{6,7},{8,9},{9,10},{10,11},{12,13},{... | collective-permute-start | bytes 24584 | tf_op jit(solution)/shard_map/ppermute | solution.py:17
  232.9 20.2 %collective-permute-start.10 = (f32[1,2,4,128]{3,2,1,0:T(4,128)S(1)}, f32[1,2,4,128]{3,2,1,0:T(4,128)S(1)}, u32[]{:S(2)}, u32[]{:S(2)}) collective-permute-start(f32[1,2,4,128]{3,2,1,0:T(4,128)S(1)} %select_bitcast_fusion.3), channel_id=1, source_target_pairs={{4,0},{8,4},{12,8},{16,12},{20,16},{24,20},{28,24},{5,1},{9,5},{13... | collective-permute-start | bytes 12296 | tf_op jit(solution)/shard_map/ppermute | solution.py:20
  236.3 16.8 %collective-permute-start.11 = (f32[1,2,4,128]{3,2,1,0:T(4,128)S(1)}, f32[1,2,4,128]{3,2,1,0:T(4,128)S(1)}, u32[]{:S(2)}, u32[]{:S(2)}) collective-permute-start(f32[1,2,4,128]{3,2,1,0:T(4,128)S(1)} %select_bitcast_fusion.2), channel_id=1, source_target_pairs={{0,4},{4,8},{8,12},{12,16},{16,20},{20,24},{24,28},{1,5},{5,9},{9,... | collective-permute-start | bytes 12296 | tf_op jit(solution)/shard_map/ppermute | solution.py:17
  244.8 8.3 %collective-permute-start.8 = (f32[1,4,4,128]{3,2,1,0:T(4,128)S(1)}, f32[1,4,4,128]{3,2,1,0:T(4,128)S(1)}, u32[]{:S(2)}, u32[]{:S(2)}) collective-permute-start(f32[1,4,4,128]{3,2,1,0:T(4,128)S(1)} %fusion.24), channel_id=1, source_target_pairs={{1,0},{2,1},{3,2},{5,4},{6,5},{7,6},{9,8},{10,9},{11,10},{13,12},{... | collective-permute-start | bytes 24584 | tf_op jit(solution)/shard_map/ppermute | solution.py:20
  250.0 3.9 %collective-permute-start.9 = (f32[1,4,4,128]{3,2,1,0:T(4,128)S(1)}, f32[1,4,4,128]{3,2,1,0:T(4,128)S(1)}, u32[]{:S(2)}, u32[]{:S(2)}) collective-permute-start(f32[1,4,4,128]{3,2,1,0:T(4,128)S(1)} %fusion.23), channel_id=1, source_target_pairs={{0,1},{1,2},{2,3},{4,5},{5,6},{6,7},{8,9},{9,10},{10,11},{12,13},{... | collective-permute-start | bytes 24584 | tf_op jit(solution)/shard_map/ppermute | solution.py:17
  299.3 20.7 %collective-permute-start.14 = (f32[1,2,4,128]{3,2,1,0:T(4,128)S(1)}, f32[1,2,4,128]{3,2,1,0:T(4,128)S(1)}, u32[]{:S(2)}, u32[]{:S(2)}) collective-permute-start(f32[1,2,4,128]{3,2,1,0:T(4,128)S(1)} %select_bitcast_fusion.1), channel_id=1, source_target_pairs={{4,0},{8,4},{12,8},{16,12},{20,16},{24,20},{28,24},{5,1},{9,5},{13... | collective-permute-start | bytes 12296 | tf_op jit(solution)/shard_map/ppermute | solution.py:20
  302.9 17.0 %collective-permute-start.15 = (f32[1,2,4,128]{3,2,1,0:T(4,128)S(1)}, f32[1,2,4,128]{3,2,1,0:T(4,128)S(1)}, u32[]{:S(2)}, u32[]{:S(2)}) collective-permute-start(f32[1,2,4,128]{3,2,1,0:T(4,128)S(1)} %select_bitcast_fusion), channel_id=1, source_target_pairs={{0,4},{4,8},{8,12},{12,16},{16,20},{20,24},{24,28},{1,5},{5,9},{9,... | collective-permute-start | bytes 12296 | tf_op jit(solution)/shard_map/ppermute | solution.py:17
  311.7 8.3 %collective-permute-start.12 = (f32[1,4,4,128]{3,2,1,0:T(4,128)S(1)}, f32[1,4,4,128]{3,2,1,0:T(4,128)S(1)}, u32[]{:S(2)}, u32[]{:S(2)}) collective-permute-start(f32[1,4,4,128]{3,2,1,0:T(4,128)S(1)} %fusion.22), channel_id=1, source_target_pairs={{1,0},{2,1},{3,2},{5,4},{6,5},{7,6},{9,8},{10,9},{11,10},{13,12},{... | collective-permute-start | bytes 24584 | tf_op jit(solution)/shard_map/ppermute | solution.py:20
  316.9 3.9 %collective-permute-start.13 = (f32[1,4,4,128]{3,2,1,0:T(4,128)S(1)}, f32[1,4,4,128]{3,2,1,0:T(4,128)S(1)}, u32[]{:S(2)}, u32[]{:S(2)}) collective-permute-start(f32[1,4,4,128]{3,2,1,0:T(4,128)S(1)} %fusion.21), channel_id=1, source_target_pairs={{0,1},{1,2},{2,3},{4,5},{5,6},{6,7},{8,9},{9,10},{10,11},{12,13},{... | collective-permute-start | bytes 24584 | tf_op jit(solution)/shard_map/ppermute | solution.py:17
where the time goes:
time: 324 us; the launch traced here: 321 us
  blocking collectives  179 us (55%)
  local copies, waits for them, and re-layouts  86 us (27%)
  starting transfers between devices  42.8 us (13%)
  matrix products  9.13 us (3%)
    psum x3, blocking collectives, project(): lax.psum((corner_local, squares), ('cluster', 'sub'))  123 us
    gather x32, local copies, waits for them, and re-layouts, permuted(): return jnp.take_along_axis(blocks, order[:, None, :], axis=2)  46 us
    psum x1, blocking collectives, apply(): lax.psum(jnp.sum(spread * product, axis=(0, 2)), ('cluster', 'sub'))  42.8 us
    scatter x2, local copies, waits for them, and re-layouts, invert(): return jnp.zeros_like(order).at[row_index, order].set(col_index)  34 us
    ppermute x8, starting transfers between devices, extended(): lax.ppermute(lax.slice_in_dim(block, block.shape[dim] - width, None, axis...  32.2 us
    psum x2, blocking collectives, project(): cluster_all, global_all = lax.psum((part_cluster, part_global), 'sub')  12.9 us
    ppermute x8, starting transfers between devices, extended(): lax.ppermute(lax.slice_in_dim(block, 0, width, axis=dim), axis, backward)  10.6 us
  transfers between devices with their start and end apart: 16, of which 3 were waited for; matrix products, arithmetic and copies ran while one was open for 23% of the time, Pallas kernels for 0%

commit v1 on v0

v1 whole, which is shorter than its diff:
```python
import functools

import jax
import jax.numpy as jnp
from jax import lax
from jax.experimental import pallas as pl
from jax.experimental.pallas import tpu as pltpu
from jax.sharding import PartitionSpec as P

ITERS = 2
LANES = 128
UNROLL = 8
MESH = pl.DeviceIdType.MESH
HIGHEST = lax.Precision.HIGHEST
NN = (((1,), (0,)), ((), ()))
NT = (((1,), (1,)), ((), ()))


def dot(a, b, dims=NN, precision=HIGHEST):
    return lax.dot_general(a, b, dims, precision=precision, preferred_element_type=jnp.float32)


def iota(shape, dim):
    return lax.broadcasted_iota(jnp.int32, shape, dim)


def each(count, body):
    if count <= UNROLL:
        for k in range(count):
            body(k)
    else:
        lax.fori_loop(0, count, lambda k, carry: (body(k), carry)[1], 0)


def total(ref, count, start):
    if count <= UNROLL:
        for k in range(count):
            start = start + ref[k]
        return start
    return lax.fori_loop(0, count, lambda k, acc: acc + ref[k], start)


def peer(axis, count, k):
    return lax.rem(lax.axis_index(axis) + k + 1, count)


class Spread:
    def __init__(self, axis, count, source, slots, send, recv, per_peer=False):
        self.axis, self.count, self.per_peer = axis, count, per_peer
        self.source, self.slots, self.send, self.recv = source, slots, send, recv

    def copy(self, k):
        target = peer(self.axis, self.count, k)
        source = self.source.at[target] if self.per_peer else self.source
        return pltpu.make_async_remote_copy(
            src_ref=source,
            dst_ref=self.slots.at[k],
            send_sem=self.send.at[k],
            recv_sem=self.recv.at[k],
            device_id={self.axis: target},
            device_id_type=MESH,
        )

    def start(self):
        each(self.count - 1, lambda k: self.copy(k).start())

    def wait_recv(self):
        each(self.count - 1, lambda k: self.copy(k).wait_recv())

    def wait_send(self):
        each(self.count - 1, lambda k: self.copy(k).wait_send())


def kernel(
    sizes,
    rhs_ref,
    operators_hbm,
    signs_ref,
    links_ref,
    cluster_basis_ref,
    corner_basis_ref,
    ids_ref,
    cluster_coarse_ref,
    global_coarse_ref,
    mult_ref,
    res_ref,
    ops_ref,
    ops_sem,
    basis_ref,
    weights_ref,
    global_ref,
    g_slots,
    g_send,
    g_recv,
    pick_ref,
    c_src,
    c_slots,
    c_send,
    c_recv,
    a_src,
    a_slots,
    a_send,
    a_recv,
    b_src,
    b_slots,
    b_send,
    b_recv,
    in_src,
    in_slots,
    in_send,
    in_recv,
    out_src,
    out_slots,
    out_send,
    out_recv,
    ka_src,
    ka_slots,
    ka_send,
    ka_recv,
    kb_src,
    kb_slots,
    kb_send,
    kb_recv,
):
    clusters, members = sizes
    subs, loads, dual = rhs_ref.shape
    rows = subs * loads
    kc, corn = cluster_basis_ref.shape[1], corner_basis_ref.shape[1]
    width = kc + corn
    coefs = subs * width
    order = global_coarse_ref.shape[1]
    solved = members * coefs
    my_c, my_s = lax.axis_index("cluster"), lax.axis_index("sub")

    fetch = pltpu.make_async_copy(operators_hbm, ops_ref, ops_sem)
    fetch.start()

    barrier = pltpu.get_barrier_semaphore()
    each(
        clusters - 1,
        lambda k: pl.semaphore_signal(
            barrier, inc=1, device_id={"cluster": peer("cluster", clusters, k)}, device_id_type=MESH
        ),
    )
    each(
        members - 1,
        lambda k: pl.semaphore_signal(
            barrier, inc=1, device_id={"sub": peer("sub", members, k)}, device_id_type=MESH
        ),
    )

    def field(ref):
        return jnp.concatenate([ref[s] for s in range(subs)], axis=0)

    rhs = field(rhs_ref)
    sign = jnp.concatenate(
        [
            jnp.broadcast_to(signs_ref[s : s + 1, :].astype(jnp.float32), (loads, dual))
            for s in range(subs)
        ],
        axis=0,
    )
    for s in range(subs):
        basis_ref[s * width : s * width + kc, :] = cluster_basis_ref[s]
        basis_ref[s * width + kc : (s + 1) * width, :] = corner_basis_ref[s]

    def row_of(s, b):
        return links_ref[s, b : b + 1, :]

    numbers = iota((8, LANES), 1).astype(jnp.bfloat16)

    def inverted(row):
        hot = (iota((LANES, LANES), 0) == row).astype(jnp.float32).astype(jnp.bfloat16)
        return dot(numbers, hot, NT, None)[:loads].astype(jnp.int32)

    def plain(row):
        return jnp.broadcast_to(row, (loads, LANES))

    up_order = jnp.concatenate([inverted(row_of(s, 0)) for s in range(subs)], axis=0)
    down_order = jnp.concatenate([plain(row_of(s, 1)) for s in range(subs)], axis=0)
    across_order = jnp.concatenate(
        [(plain if s % 2 else inverted)(row_of(s, 2)) for s in range(subs)], axis=0
    )

    id_row = jnp.full((1, coefs), -1, jnp.int32)
    lane = iota((1, coefs), 1)
    for s in range(subs):
        for c in range(corn):
            id_row = jnp.where(lane == s * width + kc + c, ids_ref[s, c], id_row)
    id_col = jnp.sum(
        jnp.where(iota((coefs, coefs), 0) == iota((coefs, coefs), 1), id_row, 0),
        axis=1,
        keepdims=True,
    )
    hot_rows = (id_col == iota((coefs, order), 1)).astype(jnp.float32)
    pick_ref[...] = (id_row == iota((order, coefs), 0)).astype(jnp.float32)

    where_to = iota((1, solved), 1)
    within = lax.rem(where_to, width)
    source = (
        (where_to // coefs) * (subs * kc) + (lax.rem(where_to, coefs) // width) * kc + within
    )
    source = jnp.where(within < kc, source, -1)
    place = (iota((members * subs * kc, solved), 0) == source).astype(jnp.float32)
    coarse = dot(cluster_coarse_ref[0], place)
    for s in range(subs):
        weights_ref[s * width : s * width + kc, :solved] = coarse[s * kc : (s + 1) * kc]
        weights_ref[s * width + kc : (s + 1) * width, :solved] = jnp.zeros(
            (corn, solved), jnp.float32
        )

    diagonal = iota((rows, coefs), 0) // loads == iota((rows, coefs), 1) // width

    def per_load(x):
        out = x[:loads]
        for s in range(1, subs):
            out = out + x[s * loads : (s + 1) * loads]
        return out

    def lanes_added(x):
        out = x[:, :LANES]
        for b in range(1, dual // LANES):
            out = out + x[:, b * LANES : (b + 1) * LANES]
        return out

    def tiled(x):
        return jnp.concatenate([x] * subs, axis=0)

    pl.semaphore_wait(barrier, clusters + members - 2)

    gather = Spread("sub", members, global_coarse_ref, g_slots, g_send, g_recv)
    gather.start()

    def place_global():
        depth = global_coarse_ref.shape[0]
        global_ref[pl.ds(pl.multiple_of(my_s * depth, 8), depth), :] = global_coarse_ref[...]
        gather.wait_recv()
        for k in range(members - 1):
            owner = lax.rem(my_s + 2 * members - k - 1, members)
            global_ref[pl.ds(pl.multiple_of(owner * depth, 8), depth), :] = g_slots[k]
        weights_ref[:, solved:] = dot(hot_rows, global_ref[...])

    def project(vector, n):
        raw = dot(vector, basis_ref[...], NT)
        coef = per_load(jnp.where(diagonal, raw, 0.0))
        squares = per_load(lanes_added(vector * vector))
        part = dot(coef, weights_ref[:, :solved])
        for j in range(members):
            c_src[n, j, :loads] = part[:, j * coefs : (j + 1) * coefs]
        solve = Spread(
            "sub", members, c_src.at[n], c_slots.at[n], c_send.at[n], c_recv.at[n], True
        )
        solve.start()
        if n == 0:
            place_global()
        part_global = dot(coef, weights_ref[:, solved:])
        a_src[n, :loads] = part_global
        a_src[n, loads:, :LANES] = squares
        if order > LANES:
            a_src[n, loads:, LANES:] = jnp.zeros((loads, order - LANES), jnp.float32)
        first = Spread("cluster", clusters, a_src.at[n], a_slots.at[n], a_send.at[n], a_recv.at[n])
        first.start()
        first.wait_recv()
        b_src[n] = total(a_slots.at[n], clusters - 1, a_src[n])
        second = Spread("sub", members, b_src.at[n], b_slots.at[n], b_send.at[n], b_recv.at[n])
        second.start()
        solve.wait_recv()
        own = c_src[n, my_s] + 0.0
        cluster_own = total(c_slots.at[n], members - 1, own)[:loads]
        second.wait_recv()
        both = total(b_slots.at[n], members - 1, b_src[n])
        norm = jnp.sum(both[loads : 2 * loads, :LANES], axis=1, keepdims=True)
        amount = cluster_own + dot(both[:loads], pick_ref[...])
        fix = dot(jnp.where(diagonal, tiled(amount), 0.0), basis_ref[...])
        return vector - fix, norm, (solve, first, second)

    def take(x, order_of):
        return jnp.take_along_axis(x, order_of, axis=1, mode="promise_in_bounds")

    def swap_copies(n):
        def one(src, slot, send, recv, axis, step):
            return pltpu.make_async_remote_copy(
                src_ref=src,
                dst_ref=slot,
                send_sem=send,
                recv_sem=recv,
                device_id={axis: lax.axis_index(axis) + step},
                device_id_type=MESH,
            )

        up = one(in_src.at[n, 0], in_slots.at[n, 0], in_send.at[n, 0], in_recv.at[n, 0], "sub", 1)
        down = one(
            in_src.at[n, 1], in_slots.at[n, 1], in_send.at[n, 1], in_recv.at[n, 1], "sub", -1
        )
        even = one(
            out_src.at[n, 0], out_slots.at[n, 0], out_send.at[n, 0], out_recv.at[n, 0], "cluster", 1
        )
        odd = one(
            out_src.at[n, 1], out_slots.at[n, 1], out_send.at[n, 1], out_recv.at[n, 1], "cluster", -1
        )
        return up, down, even, odd

    has_low, has_high = my_s > 0, my_s < members - 1
    has_prev, has_next = my_c > 0, my_c < clusters - 1

    def swap_start(x, n):
        across = take(x[:, 2 * LANES :], across_order)
        for p in range(2):
            for h in range(subs // 2):
                s = 2 * h + p
                out_src[n, p, h * loads : (h + 1) * loads] = across[s * loads : (s + 1) * loads]
        up, down, even, odd = swap_copies(n)
        pl.when(has_next)(even.start)
        pl.when(has_prev)(odd.start)
        in_src[n, 0] = take(x[:, :LANES], up_order)
        in_src[n, 1] = take(x[:, LANES : 2 * LANES], down_order)
        pl.when(has_high)(up.start)
        pl.when(has_low)(down.start)

    def swap_finish(n):
        up, down, even, odd = swap_copies(n)
        pl.when(has_low)(up.wait_recv)
        pl.when(has_high)(down.wait_recv)
        pl.when(has_prev)(even.wait_recv)
        pl.when(has_next)(odd.wait_recv)
        new_up = jnp.where(has_high, in_slots[n, 1], 0.0)
        new_down = jnp.where(has_low, in_slots[n, 0], 0.0)
        at_odd = jnp.where(has_prev, out_slots[n, 0], 0.0)
        at_even = jnp.where(has_next, out_slots[n, 1], 0.0)
        pieces = []
        for s in range(subs):
            h = s // 2
            pieces.append((at_odd if s % 2 else at_even)[h * loads : (h + 1) * loads])
        return jnp.concatenate([new_up, new_down, jnp.concatenate(pieces, axis=0)], axis=1)

    def swap_sent(n):
        up, down, even, odd = swap_copies(n)
        pl.when(has_high)(up.wait_send)
        pl.when(has_low)(down.wait_send)
        pl.when(has_next)(even.wait_send)
        pl.when(has_prev)(odd.wait_send)

    open_sends = []

    def apply(direction, n):
        swap_start(direction, 2 * n)
        if n == 0:
            fetch.wait()
        spread = sign * (direction + swap_finish(2 * n))
        spread_bf = spread.astype(jnp.bfloat16)
        image = jnp.concatenate(
            [
                dot(spread_bf[s * loads : (s + 1) * loads], ops_ref[s], NN, None)
                for s in range(subs)
            ],
            axis=0,
        )
        ka_src[n, :loads] = per_load(lanes_added(spread * image))
        first = Spread(
            "cluster", clusters, ka_src.at[n], ka_slots.at[n], ka_send.at[n], ka_recv.at[n]
        )
        first.start()
        signed = sign * image
        swap_start(signed, 2 * n + 1)
        first.wait_recv()
        kb_src[n] = total(ka_slots.at[n], clusters - 1, ka_src[n])
        second = Spread("sub", members, kb_src.at[n], kb_slots.at[n], kb_send.at[n], kb_recv.at[n])
        second.start()
        product = signed + swap_finish(2 * n + 1)
        second.wait_recv()
        both = total(kb_slots.at[n], members - 1, kb_src[n])
        open_sends.extend([first, second])
        return product, jnp.sum(both[:loads], axis=1, keepdims=True)

    residual = rhs
    direction, rho, open_spreads = project(residual, 0)
    open_sends.extend(open_spreads)
    multipliers = None
    for n in range(ITERS):
        product, curvature = apply(direction, n)
        step = tiled(rho / curvature)
        moved = step * direction
        multipliers = moved if multipliers is None else multipliers + moved
        residual = residual - step * product
        if n + 1 < ITERS:
            projected, rho_new, open_spreads = project(residual, n + 1)
            open_sends.extend(open_spreads)
            direction = projected + tiled(rho_new / rho) * direction
            rho = rho_new
    for s in range(subs):
        mult_ref[s] = multipliers[s * loads : (s + 1) * loads]
        res_ref[s] = residual[s * loads : (s + 1) * loads]
    gather.wait_send()
    for spread in open_sends:
        spread.wait_send()
    for n in range(2 * ITERS):
        swap_sent(n)


def local(sizes, rhs, operators, signs, links, cluster_basis, corner_basis, ids, coarse, glob):
    clusters, members = sizes
    subs, loads, dual = rhs.shape
    coefs = subs * (cluster_basis.shape[1] + corner_basis.shape[1])
    depth, order = glob.shape
    f32 = jnp.float32
    dma = pltpu.SemaphoreType.DMA

    def spread_scratch(count, peers, block, send_block=None):
        return [
            pltpu.VMEM((count,) + (send_block or block), f32),
            pltpu.VMEM((count, peers) + block, f32),
            dma((count, peers)),
            dma((count, peers)),
        ]

    vmem = pl.BlockSpec(memory_space=pltpu.VMEM)
    scratch = [
        pltpu.VMEM(operators.shape, operators.dtype),
        dma(()),
        pltpu.VMEM((coefs, dual), f32),
        pltpu.VMEM((coefs, members * coefs + order), f32),
        pltpu.VMEM((order, order), f32),
        pltpu.VMEM((members - 1, depth, order), f32),
        dma((members - 1,)),
        dma((members - 1,)),
        pltpu.VMEM((order, coefs), f32),
    ]
    scratch += spread_scratch(ITERS, members - 1, (loads, coefs), (members, loads, coefs))
    scratch += spread_scratch(ITERS, clusters - 1, (2 * loads, order))
    scratch += spread_scratch(ITERS, members - 1, (2 * loads, order))
    scratch += [
        pltpu.VMEM((2 * ITERS, 2, subs * loads, LANES), f32),
        pltpu.VMEM((2 * ITERS, 2, subs * loads, LANES), f32),
        dma((2 * ITERS, 2)),
        dma((2 * ITERS, 2)),
        pltpu.VMEM((2 * ITERS, 2, subs * loads // 2, LANES), f32),
        pltpu.VMEM((2 * ITERS, 2, subs * loads // 2, LANES), f32),
        dma((2 * ITERS, 2)),
        dma((2 * ITERS, 2)),
    ]
    scratch += spread_scratch(ITERS, clusters - 1, (loads, LANES))
    scratch += spread_scratch(ITERS, members - 1, (loads, LANES))
    return pl.pallas_call(
        functools.partial(kernel, sizes),
        out_shape=[jax.ShapeDtypeStruct(rhs.shape, f32)] * 2,
        in_specs=[
            vmem,
            pl.BlockSpec(memory_space=pl.ANY),
            vmem,
            vmem,
            vmem,
            vmem,
            pl.BlockSpec(memory_space=pltpu.SMEM),
            vmem,
            vmem,
        ],
        out_specs=[vmem, vmem],
        scratch_shapes=scratch,
        compiler_params=pltpu.CompilerParams(collective_id=0, has_side_effects=True),
    )(rhs, operators, signs, links, cluster_basis, corner_basis, ids, coarse, glob)


def solution(mesh):
    placed = (
        P(("cluster", "sub"), None, None),
        P(("cluster", "sub"), None, None),
        P(("cluster", "sub"), None),
        P(("cluster", "sub"), None, None),
        P(("cluster", "sub"), None, None),
        P(("cluster", "sub"), None, None),
        P(("cluster", "sub"), None),
        P("cluster", "sub", None),
        P("sub", None),
    )
    return jax.shard_map(
        functools.partial(local, (mesh.shape["cluster"], mesh.shape["sub"])),
        mesh=mesh,
        in_specs=placed,
        out_specs=(P(("cluster", "sub"), None, None), P(("cluster", "sub"), None, None)),
        check_vma=False,
    )
```

time: 324 us -> 51.9 us (0.16)
  blocking collectives: 179 us -> 0 us
  local copies, waits for them, and re-layouts: 86 us -> 3.99 us
  Pallas kernels: 0 us -> 47 us
  starting transfers between devices: 42.8 us -> 0 us
  matrix products: 9.13 us -> 0 us
    psum x6 -> x0, blocking collectives: 179 us -> none  [the longest x3 123 us: project(): lax.psum((corner_local, squares), ('cluster', 'sub'))]
    gather x34 -> x0, local copies, waits for them, and re-layouts: 47.2 us -> none  [the longest x32 46 us: permuted(): return jnp.take_along_axis(blocks, order[:, None, :], axis=2)]
    pallas_call x0 -> x1, Pallas kernels: none -> 47 us  [local(): pl.pallas_call(functools.partial(kernel, sizes), out_shape=[jax.ShapeDtyp...]
    ppermute x16 -> x0, starting transfers between devices: 42.8 us -> none  [the longest x8 32.2 us: extended(): lax.ppermute(lax.slice_in_dim(block, block.shape[dim] - width, None, axis...]
    scatter x2 -> x0, local copies, waits for them, and re-layouts: 34 us -> none  [invert(): return jnp.zeros_like(order).at[row_index, order].set(col_index)]
    dot_general x16 -> x0, matrix products: 9.13 us -> none  [the longest x2 1.51 us: project(): jnp.einsum('srl,skl->srk', vector, cluster_basis, precision=HIGHEST_PRECI...]
    unnamed x16 -> x3, local copies, waits for them, and re-layouts: 0.05 us -> 3.99 us
  transfers between devices with their start and end apart: 16 -> 0, of which waited for: 3 -> 0; matrix products, arithmetic and copies ran while one was open for 23% -> 0% of each run, Pallas kernels for 0% -> 0%
where the time goes in v1:
time: 51.9 us; the launch traced here: 51.6 us
  Pallas kernels  47 us (91%)
  local copies, waits for them, and re-layouts  3.99 us (8%)
  between operations  0.64 us (1%)
    pallas_call x1, Pallas kernels, local(): pl.pallas_call(functools.partial(kernel, sizes), out_shape=[jax.ShapeDtyp...  47 us
    unnamed x3, local copies, waits for them, and re-layouts  3.99 us

profile of v1, /device:TPU:0, one launch (start us, length us, event | category | flops | bytes accessed | tf_op | source)
XLA Modules:
  0.0 51.6 jit_solution(16010054875940846300)
XLA Ops:
  0.6 1.3 %copy.11.links_ref = s32[4,3,128]{2,1,0:T(4,128)} copy(s32[4,3,128]{2,0,1:T(4,128)} %param.12) | data formatting | bytes 12288 | tf_op args[3]
  1.9 47.0 %shard_map.104 = (f32[4,4,384]{2,1,0:T(4,128)}, f32[4,4,384]{2,1,0:T(4,128)}) custom-call(f32[4,4,384]{2,1,0:T(4,128)} %rhs_ref.1, bf16[4,384,384]{2,1,0:T(8,128)(2,1)} %operators_hbm.1, s32[4,384]{1,0:T(4,128)} %signs_ref.1, s32[4,3,128]{2,1,0:T(4,128)} %copy.11.links_ref, f32[4,24,384]{2,1,0:T(8,128)} %cluster_basis_ref.1, f32[4,8,384]{2,1,0:T(8,128)} %corner_basis_ref.1, ...), custom_call_target="tpu_custom_call" | custom-call | tf_op jit(solution)/shard_map/pallas_call | solution.py:443
  48.9 1.3 %copy.14 = f32[4,4,384]{2,1,0:T(4,128)} copy(f32[4,4,384]{2,1,0:T(4,128)} %get-tuple-element.4) | data formatting | bytes 49152
  50.3 1.3 %copy.15 = f32[4,4,384]{2,1,0:T(4,128)} copy(f32[4,4,384]{2,1,0:T(4,128)} %get-tuple-element.5) | data formatting | bytes 49152

commit v2 on v0

v2 whole, which is shorter than its diff:
```python
import functools

import jax
import jax.numpy as jnp
from jax import lax
from jax.experimental import pallas as pl
from jax.experimental.pallas import tpu as pltpu
from jax.sharding import PartitionSpec as P

ITERS = 2
LANES = 128
UNROLL = 32
MESH = pl.DeviceIdType.MESH
HIGHEST = lax.Precision.HIGHEST
NN = (((1,), (0,)), ((), ()))
NT = (((1,), (1,)), ((), ()))


def dot(a, b, dims=NN, precision=HIGHEST):
    return lax.dot_general(a, b, dims, precision=precision, preferred_element_type=jnp.float32)


def iota(shape, dim):
    return lax.broadcasted_iota(jnp.int32, shape, dim)


def each(count, body):
    if count <= UNROLL:
        for k in range(count):
            body(k)
    else:
        lax.fori_loop(0, count, lambda k, carry: (body(k), carry)[1], 0)


def total(ref, count, start):
    if count <= UNROLL:
        terms = [start] + [ref[k] for k in range(count)]
        while len(terms) > 1:
            terms = [sum(terms[i : i + 2][1:], terms[i]) for i in range(0, len(terms), 2)]
        return terms[0]
    return lax.fori_loop(0, count, lambda k, acc: acc + ref[k], start)


class Spread:
    def __init__(self, sizes, axes, source, slots, send, recv):
        self.sizes, self.axes = sizes, axes
        self.source, self.slots, self.send, self.recv = source, slots, send, recv
        self.count = peers_of(sizes, axes)

    def copy(self, k):
        return pltpu.make_async_remote_copy(
            src_ref=self.source,
            dst_ref=self.slots.at[k],
            send_sem=self.send.at[k],
            recv_sem=self.recv.at[k],
            device_id=peer(self.sizes, self.axes, k),
            device_id_type=MESH,
        )

    def start(self):
        each(self.count, lambda k: self.copy(k).start())

    def wait_recv(self):
        each(self.count, lambda k: self.copy(k).wait_recv())

    def wait_send(self):
        each(self.count, lambda k: self.copy(k).wait_send())


def peers_of(sizes, axes):
    clusters, members = sizes
    return {"both": clusters * members, "cluster": clusters, "sub": members}[axes] - 1


def peer(sizes, axes, k):
    clusters, members = sizes
    if axes == "both":
        c, m = (k + 1) // members, (k + 1) % members
        return {
            "cluster": lax.rem(lax.axis_index("cluster") + c, clusters),
            "sub": lax.rem(lax.axis_index("sub") + m, members),
        }
    count = clusters if axes == "cluster" else members
    return {axes: lax.rem(lax.axis_index(axes) + k + 1, count)}


def stages(sizes):
    return ("both",) if sizes[0] * sizes[1] <= UNROLL else ("cluster", "sub")


class AllSum:
    def __init__(self, sizes, refs, n):
        self.spreads = []
        for i, axes in enumerate(stages(sizes)):
            source, slots, send, recv = refs[4 * i : 4 * i + 4]
            self.spreads.append(
                Spread(sizes, axes, source.at[n], slots.at[n], send.at[n], recv.at[n])
            )

    def start(self):
        self.spreads[0].start()

    def finish(self):
        for i, spread in enumerate(self.spreads):
            spread.wait_recv()
            out = total(spread.slots, spread.count, spread.source[...])
            if i + 1 < len(self.spreads):
                self.spreads[i + 1].source[...] = out
                self.spreads[i + 1].start()
        return out

    def wait_send(self):
        for spread in self.spreads:
            spread.wait_send()


def kernel(sizes, *refs):
    clusters, members = sizes
    hbm, out_ref, refs = refs[:9], refs[9], list(refs[10:])

    def take_refs(count):
        taken = refs[:count]
        del refs[:count]
        return taken

    local_refs = take_refs(9)
    (
        rhs_ref,
        ops_ref,
        signs_ref,
        links_ref,
        cluster_basis_ref,
        corner_basis_ref,
        ids_ref,
        cluster_coarse_ref,
        global_coarse_ref,
    ) = local_refs
    (local_sem,) = take_refs(1)
    basis_ref, weights_ref, global_ref, picked_ref, swapped_basis_ref = take_refs(5)
    g_send, g_recv = take_refs(2)
    part_refs = take_refs(4)
    piece_slots, piece_send, piece_recv = take_refs(3)
    tail_refs = take_refs(4 * len(stages(sizes)))
    curve_refs = take_refs(4 * len(stages(sizes)))
    swap_refs = take_refs(8)
    table_refs = take_refs(8)

    subs, loads, dual = rhs_ref.shape
    rows = subs * loads
    kc, corn = cluster_basis_ref.shape[1], corner_basis_ref.shape[1]
    width = kc + corn
    coefs = subs * width
    order = global_coarse_ref.shape[1]
    solved = members * coefs
    my_c, my_s = lax.axis_index("cluster"), lax.axis_index("sub")
    has_low, has_high = my_s > 0, my_s < members - 1
    has_prev, has_next = my_c > 0, my_c < clusters - 1

    barrier = pltpu.get_barrier_semaphore()

    def greet(device_id):
        pl.semaphore_signal(barrier, inc=1, device_id=device_id, device_id_type=MESH)

    greeted = 0
    for axes in ("both",) if len(stages(sizes)) == 1 else ("cluster", "sub"):
        count = peers_of(sizes, axes)
        each(count, lambda k, axes=axes: greet(peer(sizes, axes, k)))
        greeted += count
    if len(stages(sizes)) > 1:
        for there, step in ((has_next, 1), (has_prev, -1)):

            @pl.when(there)
            def _():
                for m in range(1, members):
                    greet({"cluster": my_c + step, "sub": lax.rem(my_s + m, members)})

            greeted = greeted + there.astype(jnp.int32) * (members - 1)

    loads_in = [
        pltpu.make_async_copy(hbm[i], local_refs[i], local_sem.at[i]) for i in range(len(hbm))
    ]
    for i in (6, 5, 4, 0, 7, 8, 3, 2, 1):
        loads_in[i].start()
    numbers = iota((8, LANES), 1).astype(jnp.bfloat16)

    loads_in[6].wait()
    id_row = jnp.full((1, coefs), -1, jnp.int32)
    lane = iota((1, coefs), 1)
    for s in range(subs):
        for c in range(corn):
            id_row = jnp.where(lane == s * width + kc + c, ids_ref[s, c], id_row)
    id_col = jnp.sum(
        jnp.where(iota((coefs, coefs), 0) == iota((coefs, coefs), 1), id_row, 0),
        axis=1,
        keepdims=True,
    )
    weights_ref[:, solved:] = (id_col == iota((coefs, order), 1)).astype(jnp.float32)

    loads_in[5].wait()
    loads_in[4].wait()
    for s in range(subs):
        basis_ref[s * width : s * width + kc, :] = cluster_basis_ref[s]
        basis_ref[s * width + kc : (s + 1) * width, :] = corner_basis_ref[s]

    where_to = iota((1, solved), 1)
    within = lax.rem(where_to, width)
    source = (where_to // coefs) * (subs * kc) + (lax.rem(where_to, coefs) // width) * kc + within
    source = jnp.where(within < kc, source, -1)
    place = (iota((members * subs * kc, solved), 0) == source).astype(jnp.float32)
    loads_in[0].wait()
    loads_in[7].wait()
    coarse = dot(cluster_coarse_ref[0], place)
    for s in range(subs):
        weights_ref[s * width : s * width + kc, :solved] = coarse[s * kc : (s + 1) * kc]
        weights_ref[s * width + kc : (s + 1) * width, :solved] = jnp.zeros(
            (corn, solved), jnp.float32
        )

    diagonal = iota((rows, coefs), 0) // loads == iota((rows, coefs), 1) // width
    row_sub, lane_sub = iota((rows, coefs), 0) // loads, iota((rows, coefs), 1) // width
    crossed = row_sub + 1 - 2 * lax.rem(row_sub, 2) == lane_sub

    def per_load(x):
        out = x[:loads]
        for s in range(1, subs):
            out = out + x[s * loads : (s + 1) * loads]
        return out

    def lanes_added(x):
        out = x[:, :LANES]
        for b in range(1, dual // LANES):
            out = out + x[:, b * LANES : (b + 1) * LANES]
        return out

    def tiled(x):
        return jnp.concatenate([x] * subs, axis=0)

    open_sends = []

    def piece_copy(n, side, k, step):
        target = lax.rem(my_s + k, members)
        return pltpu.make_async_remote_copy(
            src_ref=part_refs[0].at[n, target],
            dst_ref=piece_slots.at[n, side, k],
            send_sem=piece_send.at[n, side, k],
            recv_sem=piece_recv.at[n, side, k],
            device_id={"cluster": my_c + step, "sub": target},
            device_id_type=MESH,
        )

    def pieces(n, side, what):
        step = 1 - 2 * side
        for k in range(members):
            getattr(piece_copy(n, side, k, step), what)()

    def project_start(vector, n):
        raw = dot(vector, basis_ref[...], NT)
        coef = per_load(jnp.where(diagonal, raw, 0.0))
        both = dot(coef, weights_ref[...])
        tail_refs[0][n, :loads] = both[:, solved:]
        tail_refs[0][n, loads:, :LANES] = per_load(lanes_added(vector * vector))
        if order > LANES:
            tail_refs[0][n, loads:, LANES:] = jnp.zeros((loads, order - LANES), jnp.float32)
        for j in range(members):
            part_refs[0][n, j] = both[:, j * coefs : (j + 1) * coefs]
        tail = AllSum(sizes, tail_refs, n)
        tail.start()
        part = Spread(sizes, "sub", *[ref.at[n] for ref in part_refs])
        part.start()
        pl.when(has_next)(lambda: pieces(n, 0, "start"))
        pl.when(has_prev)(lambda: pieces(n, 1, "start"))
        return tail, part

    def project_finish(n, tail, part):
        part.wait_recv()
        pl.when(has_prev)(lambda: pieces(n, 0, "wait_recv"))
        pl.when(has_next)(lambda: pieces(n, 1, "wait_recv"))

        def cluster_of(member):
            out = part_refs[0][n, member]
            for k in range(members - 1):
                out = out + part_refs[1][n, k, member]
            return out

        def piece_sum(side):
            return total(piece_slots.at[n, side], members - 1, piece_slots[n, side, members - 1])

        own = cluster_of(my_s)
        high = cluster_of(jnp.minimum(my_s + 1, members - 1))
        low = cluster_of(jnp.maximum(my_s - 1, 0))
        prev, following = piece_sum(0), piece_sum(1)
        summed = tail.finish()
        open_sends.extend([tail, part])
        norm = jnp.sum(summed[loads:, :LANES], axis=1, keepdims=True)
        corners = dot(summed[:loads], picked_ref[...])

        def amount(base, i):
            return base + corners[:, i * coefs : (i + 1) * coefs]

        def block_diagonal(x, mask):
            return jnp.where(mask, tiled(x), 0.0)

        fix = dot(block_diagonal(amount(own, 0), diagonal), basis_ref[...])
        high = jnp.where(has_high, amount(high, 1), 0.0)
        low = jnp.where(has_low, amount(low, 2), 0.0)
        following = jnp.where(has_next, amount(following, 3), 0.0)
        prev = jnp.where(has_prev, amount(prev, 4), 0.0)
        odd = lax.rem(iota((loads, coefs), 1) // width, 2) == 1
        cross = jnp.where(odd, following, prev)
        fix_swapped = jnp.concatenate(
            [
                dot(block_diagonal(high, diagonal), swapped_basis_ref[0]),
                dot(block_diagonal(low, diagonal), swapped_basis_ref[1]),
                dot(block_diagonal(cross, crossed), swapped_basis_ref[2]),
            ],
            axis=1,
        )
        return fix, fix_swapped, norm

    def take(x, order_of):
        return jnp.take_along_axis(x, order_of, axis=1, mode="promise_in_bounds")

    class Swap:
        def __init__(self, refs, n):
            in_src, in_slots, in_send, in_recv, out_src, out_slots, out_send, out_recv = refs
            self.sources = [in_src.at[n, 0], in_src.at[n, 1], out_src.at[n, 0], out_src.at[n, 1]]
            self.slots = [
                in_slots.at[n, 0],
                in_slots.at[n, 1],
                out_slots.at[n, 0],
                out_slots.at[n, 1],
            ]
            self.send = [in_send.at[n, 0], in_send.at[n, 1], out_send.at[n, 0], out_send.at[n, 1]]
            self.recv = [in_recv.at[n, 0], in_recv.at[n, 1], out_recv.at[n, 0], out_recv.at[n, 1]]
            self.sends = [has_high, has_low, has_next, has_prev]
            self.takes = [has_low, has_high, has_prev, has_next]

        def copy(self, i):
            axis = "sub" if i < 2 else "cluster"
            return pltpu.make_async_remote_copy(
                src_ref=self.sources[i],
                dst_ref=self.slots[i],
                send_sem=self.send[i],
                recv_sem=self.recv[i],
                device_id={axis: lax.axis_index(axis) + (-1 if i % 2 else 1)},
                device_id_type=MESH,
            )

        def start(self, x, orders, height, extra=None):
            up_order, down_order, across_order = orders
            count = subs * height
            across = take(x[:, 2 * LANES :], across_order)
            for p in range(2):
                for h in range(subs // 2):
                    s = 2 * h + p
                    self.sources[2 + p][h * height : (h + 1) * height] = across[
                        s * height : (s + 1) * height
                    ]
            self.sources[0][:count] = take(x[:, :LANES], up_order)
            self.sources[1][:count] = take(x[:, LANES : 2 * LANES], down_order)
            if extra is not None:
                for i in range(4):
                    first = count if i < 2 else count // 2
                    self.sources[i][first : first + 8] = extra
            for i in (2, 3, 0, 1):
                pl.when(self.sends[i])(self.copy(i).start)

        def wait_recv(self):
            for i in range(4):
                pl.when(self.takes[i])(self.copy(i).wait_recv)

        def wait_send(self):
            for i in range(4):
                pl.when(self.sends[i])(self.copy(i).wait_send)

        def arrived(self, i):
            return jnp.where(self.takes[i], self.slots[i][...], 0.0)

        def field(self):
            self.wait_recv()
            at_odd, at_even = self.arrived(2), self.arrived(3)
            across = [
                (at_odd if s % 2 else at_even)[s // 2 * loads : (s // 2 + 1) * loads]
                for s in range(subs)
            ]
            return jnp.concatenate(
                [self.arrived(1), self.arrived(0), jnp.concatenate(across, axis=0)], axis=1
            )

    depth = global_coarse_ref.shape[0]
    own_rows = pl.ds(pl.multiple_of(my_s * depth, 8), depth)

    def gather_copy(k):
        return pltpu.make_async_remote_copy(
            src_ref=global_coarse_ref,
            dst_ref=global_ref.at[own_rows],
            send_sem=g_send.at[k],
            recv_sem=g_recv.at[k],
            device_id=peer(sizes, "sub", k),
            device_id_type=MESH,
        )

    def begin():
        loads_in[8].wait()
        global_ref[own_rows, :] = global_coarse_ref[...]
        each(members - 1, lambda k: gather_copy(k).start())
        loads_in[3].wait()

        def plain(row):
            return row

        def inverted(row):
            hot = (iota((LANES, LANES), 0) == row).astype(jnp.float32).astype(jnp.bfloat16)
            return dot(numbers, hot, NT, None)[:1].astype(jnp.int32)

        index = [
            [inverted(links_ref[0, s : s + 1, :]) for s in range(subs)],
            [plain(links_ref[1, s : s + 1, :]) for s in range(subs)],
            [(plain if s % 2 else inverted)(links_ref[2, s : s + 1, :]) for s in range(subs)],
        ]

        def orders_of(height):
            return [
                jnp.concatenate(
                    [jnp.broadcast_to(row, (height, LANES)) for row in block], axis=0
                )
                for block in index
            ]

        orders = orders_of(loads)
        rhs_swap = Swap(swap_refs, ITERS)
        rhs_swap.start(rhs, orders, loads)
        tables = Swap(table_refs, 0)
        ids_sent = jnp.broadcast_to(id_row.astype(jnp.float32), (8, coefs))
        tables.start(basis_ref[...], orders_of(width), width, ids_sent)

        loads_in[2].wait()
        sign = jnp.concatenate(
            [
                jnp.broadcast_to(signs_ref[s : s + 1, :].astype(jnp.float32), (loads, dual))
                for s in range(subs)
            ],
            axis=0,
        )
        each(members - 1, lambda k: gather_copy(k).wait_recv())
        tables.wait_recv()
        swapped_basis_ref[0] = tables.arrived(1)[:coefs]
        swapped_basis_ref[1] = tables.arrived(0)[:coefs]
        from_prev, from_next = tables.arrived(2), tables.arrived(3)
        for s in range(subs):
            swapped_basis_ref[2, s * width : (s + 1) * width] = (
                from_next if s % 2 else from_prev
            )[s // 2 * width : (s // 2 + 1) * width]
        id_rows = [id_row.astype(jnp.float32)]
        for i in (1, 0, 3, 2):
            first = coefs if i < 2 else coefs // 2
            id_rows.append(tables.slots[i][first : first + 1])
        whose = iota((order, coefs), 0).astype(jnp.float32)
        picks = jnp.concatenate([(row == whose).astype(jnp.float32) for row in id_rows], axis=1)
        for r in range(0, order, 2 * LANES):
            chunk = slice(r, min(r + 2 * LANES, order))
            picked_ref[chunk] = dot(global_ref[chunk], picks)
        loads_in[1].wait()
        open_sends.extend([rhs_swap, tables])
        return sign, orders, rhs_swap.field()

    rhs = jnp.concatenate([rhs_ref[s] for s in range(subs)], axis=0)
    pl.semaphore_wait(barrier, greeted)
    started = project_start(rhs, 0)
    sign, orders, residual_swapped = begin()
    fix, fix_swapped, rho = project_finish(0, *started)
    residual = rhs
    direction, direction_swapped = residual - fix, residual_swapped - fix_swapped
    row_odd = lax.rem(iota((rows, LANES), 0) // loads, 2) == 1
    there = jnp.concatenate(
        [
            jnp.full((rows, LANES), has_high.astype(jnp.float32)),
            jnp.full((rows, LANES), has_low.astype(jnp.float32)),
            jnp.where(row_odd, has_prev.astype(jnp.float32), has_next.astype(jnp.float32)),
        ],
        axis=1,
    )
    multipliers = None
    for n in range(ITERS):
        spread = sign * (direction + direction_swapped)
        spread_bf = spread.astype(jnp.bfloat16)
        image = jnp.concatenate(
            [
                dot(spread_bf[s * loads : (s + 1) * loads], ops_ref[s], NN, None)
                for s in range(subs)
            ],
            axis=0,
        )
        curve_refs[0][n] = per_load(lanes_added(spread * image))
        curve = AllSum(sizes, curve_refs, n)
        curve.start()
        signed = sign * image
        swap = Swap(swap_refs, n)
        swap.start(signed, orders, loads)
        signed_swapped = swap.field()
        product = signed + signed_swapped
        product_swapped = signed_swapped + there * signed
        curvature = jnp.sum(curve.finish(), axis=1, keepdims=True)
        open_sends.extend([curve, swap])
        step = tiled(rho / curvature)
        residual = residual - step * product
        if n + 1 < ITERS:
            started = project_start(residual, n + 1)
        moved = step * direction
        multipliers = moved if multipliers is None else multipliers + moved
        if n + 1 < ITERS:
            residual_swapped = residual_swapped - step * product_swapped
            fix, fix_swapped, rho_new = project_finish(n + 1, *started)
            ratio = tiled(rho_new / rho)
            direction = residual - fix + ratio * direction
            direction_swapped = residual_swapped - fix_swapped + ratio * direction_swapped
            rho = rho_new
    for s in range(subs):
        out_ref[0, s] = multipliers[s * loads : (s + 1) * loads]
        out_ref[1, s] = residual[s * loads : (s + 1) * loads]
    for spread in open_sends:
        spread.wait_send()
    each(members - 1, lambda k: gather_copy(k).wait_send())
    for n in range(ITERS):
        pl.when(has_next)(lambda n=n: pieces(n, 0, "wait_send"))
        pl.when(has_prev)(lambda n=n: pieces(n, 1, "wait_send"))


def split(both_ref, mult_ref, res_ref):
    mult_ref[...] = both_ref[0]
    res_ref[...] = both_ref[1]


def local(sizes, *args):
    args = list(args)
    args[3] = jnp.transpose(args[3], (1, 0, 2))
    rhs, operators, signs, links, cluster_basis, corner_basis, ids, coarse, glob = args
    clusters, members = sizes
    subs, loads, dual = rhs.shape
    coefs = subs * (cluster_basis.shape[1] + corner_basis.shape[1])
    depth, order = glob.shape
    f32 = jnp.float32
    dma = pltpu.SemaphoreType.DMA

    def exchange(lead, block, receive):
        return [
            pltpu.VMEM(lead[:1] + block, f32),
            pltpu.VMEM(lead + receive, f32),
            dma(lead),
            dma(lead),
        ]

    def swap_scratch(count, height, extra):
        scratch = []
        for rows in (subs * height + extra, subs * height // 2 + extra):
            scratch += [
                pltpu.VMEM((count, 2, rows, LANES), f32),
                pltpu.VMEM((count, 2, rows, LANES), f32),
                dma((count, 2)),
                dma((count, 2)),
            ]
        return scratch

    def sum_scratch(block):
        scratch = []
        for axes in stages(sizes):
            scratch += exchange((ITERS, peers_of(sizes, axes)), block, block)
        return scratch

    vmem = pl.BlockSpec(memory_space=pltpu.VMEM)
    scratch = [pltpu.VMEM(a.shape, a.dtype) for a in args]
    scratch[6] = pltpu.SMEM(ids.shape, ids.dtype)
    scratch += [
        dma((len(args),)),
        pltpu.VMEM((coefs, dual), f32),
        pltpu.VMEM((coefs, members * coefs + order), f32),
        pltpu.VMEM((order, order), f32),
        pltpu.VMEM((order, 5 * coefs), f32),
        pltpu.VMEM((3, coefs, LANES), f32),
        dma((members - 1,)),
        dma((members - 1,)),
    ]
    part = (members, loads, coefs)
    scratch += exchange((ITERS, members - 1), part, part)
    scratch += [
        pltpu.VMEM((ITERS, 2, members, loads, coefs), f32),
        dma((ITERS, 2, members)),
        dma((ITERS, 2, members)),
    ]
    scratch += sum_scratch((2 * loads, order)) + sum_scratch((loads, LANES))
    scratch += swap_scratch(ITERS + 1, loads, 0)
    scratch += swap_scratch(1, coefs // subs, 8)
    both = pl.pallas_call(
        functools.partial(kernel, sizes),
        out_shape=jax.ShapeDtypeStruct((2,) + rhs.shape, f32),
        in_specs=[pl.BlockSpec(memory_space=pl.ANY)] * len(args),
        out_specs=vmem,
        scratch_shapes=scratch,
        compiler_params=pltpu.CompilerParams(collective_id=0, has_side_effects=True),
    )(*args)
    return pl.pallas_call(
        split,
        out_shape=[jax.ShapeDtypeStruct(rhs.shape, f32)] * 2,
        in_specs=[vmem],
        out_specs=[vmem, vmem],
    )(both)


def solution(mesh):
    placed = (
        P(("cluster", "sub"), None, None),
        P(("cluster", "sub"), None, None),
        P(("cluster", "sub"), None),
        P(("cluster", "sub"), None, None),
        P(("cluster", "sub"), None, None),
        P(("cluster", "sub"), None, None),
        P(("cluster", "sub"), None),
        P("cluster", "sub", None),
        P("sub", None),
    )
    return jax.shard_map(
        functools.partial(local, (mesh.shape["cluster"], mesh.shape["sub"])),
        mesh=mesh,
        in_specs=placed,
        out_specs=(P(("cluster", "sub"), None, None), P(("cluster", "sub"), None, None)),
        check_vma=False,
    )
```

time: 324 us -> 37.2 us (0.11)
  blocking collectives: 179 us -> 0 us
  local copies, waits for them, and re-layouts: 86 us -> 0 us
  starting transfers between devices: 42.8 us -> 0 us
  Pallas kernels: 0 us -> 36.4 us
  matrix products: 9.13 us -> 0 us
    psum x6 -> x0, blocking collectives: 179 us -> none  [the longest x3 123 us: project(): lax.psum((corner_local, squares), ('cluster', 'sub'))]
    gather x34 -> x0, local copies, waits for them, and re-layouts: 47.2 us -> none  [the longest x32 46 us: permuted(): return jnp.take_along_axis(blocks, order[:, None, :], axis=2)]
    ppermute x16 -> x0, starting transfers between devices: 42.8 us -> none  [the longest x8 32.2 us: extended(): lax.ppermute(lax.slice_in_dim(block, block.shape[dim] - width, None, axis...]
    pallas_call x0 -> x2, Pallas kernels: none -> 36.4 us  [the longest x1 34.9 us: local(): pl.pallas_call(functools.partial(kernel, sizes), out_shape=jax.ShapeDtype...]
    scatter x2 -> x0, local copies, waits for them, and re-layouts: 34 us -> none  [invert(): return jnp.zeros_like(order).at[row_index, order].set(col_index)]
    dot_general x16 -> x0, matrix products: 9.13 us -> none  [the longest x2 1.51 us: project(): jnp.einsum('srl,skl->srk', vector, cluster_basis, precision=HIGHEST_PRECI...]
  transfers between devices with their start and end apart: 16 -> 0, of which waited for: 3 -> 0; matrix products, arithmetic and copies ran while one was open for 23% -> 0% of each run, Pallas kernels for 0% -> 0%
where the time goes in v2:
time: 37.2 us; the launch traced here: 37 us
  Pallas kernels  36.4 us (98%)
  between operations  0.64 us (2%)
    pallas_call x1, Pallas kernels, local(): pl.pallas_call(functools.partial(kernel, sizes), out_shape=jax.ShapeDtype...  34.9 us
    pallas_call x1, Pallas kernels, local(): pl.pallas_call(split, out_shape=[jax.ShapeDtypeStruct(rhs.shape, f32)] *...  1.42 us

profile of v2, /device:TPU:0, one launch (start us, length us, event | category | flops | bytes accessed | tf_op | source)
XLA Modules:
  0.0 37.0 jit_solution(2858502120160390267)
XLA Ops:
  0.6 34.9 %shard_map.104.both_ref = f32[2,4,4,384]{3,2,1,0:T(4,128)} custom-call(f32[4,4,384]{2,1,0:T(4,128)} %refs_0_.1, bf16[4,384,384]{2,1,0:T(8,128)(2,1)} %refs_1_.1, s32[4,384]{1,0:T(4,128)} %refs_2_.1, s32[3,4,128]{2,1,0:T(4,128)} %bitcast.1, f32[4,24,384]{2,1,0:T(8,128)} %refs_4_.1, f32[4,8,384]{2,1,0:T(8,128)} %refs_5_.1, s32[4,8]{1,0:T(4,128)} %refs_6_.1, ...), custom_call_target="tpu_custom_call" | custom-call | tf_op jit(solution)/shard_map/pallas_call | solution.py:593
  35.6 1.4 %shard_map.105 = (f32[4,4,384]{2,1,0:T(4,128)}, f32[4,4,384]{2,1,0:T(4,128)}) custom-call(f32[2,4,4,384]{3,2,1,0:T(4,128)} %shard_map.104.both_ref), custom_call_target="tpu_custom_call" | custom-call | tf_op jit(solution)/shard_map/pallas_call | solution.py:601

commit v3 on v2

--- a/solution.py
+++ b/solution.py
@@ -235,6 +235,15 @@
     def tiled(x):
         return jnp.concatenate([x] * subs, axis=0)
 
+    lane_is_load = iota((loads, LANES), 0) == iota((loads, LANES), 1)
+
+    def as_row(x):
+        sums = jnp.sum(x, axis=1, keepdims=True)
+        return jnp.sum(jnp.where(lane_is_load, sums, 0.0), axis=0, keepdims=True)
+
+    def as_column(x):
+        return jnp.sum(jnp.where(lane_is_load, x, 0.0), axis=1, keepdims=True)
+
     open_sends = []
 
     def piece_copy(n, side, k, step):
@@ -258,9 +267,9 @@
         coef = per_load(jnp.where(diagonal, raw, 0.0))
         both = dot(coef, weights_ref[...])
         tail_refs[0][n, :loads] = both[:, solved:]
-        tail_refs[0][n, loads:, :LANES] = per_load(lanes_added(vector * vector))
+        tail_refs[0][n, loads:, :LANES] = as_row(per_load(lanes_added(vector * vector)))
         if order > LANES:
-            tail_refs[0][n, loads:, LANES:] = jnp.zeros((loads, order - LANES), jnp.float32)
+            tail_refs[0][n, loads:, LANES:] = jnp.zeros((1, order - LANES), jnp.float32)
         for j in range(members):
             part_refs[0][n, j] = both[:, j * coefs : (j + 1) * coefs]
         tail = AllSum(sizes, tail_refs, n)
@@ -291,7 +300,7 @@
         prev, following = piece_sum(0), piece_sum(1)
         summed = tail.finish()
         open_sends.extend([tail, part])
-        norm = jnp.sum(summed[loads:, :LANES], axis=1, keepdims=True)
+        norm = as_column(summed[loads:, :LANES])
         corners = dot(summed[:loads], picked_ref[...])
 
         def amount(base, i):
@@ -491,7 +500,7 @@
             ],
             axis=0,
         )
-        curve_refs[0][n] = per_load(lanes_added(spread * image))
+        curve_refs[0][n] = as_row(per_load(lanes_added(spread * image)))
         curve = AllSum(sizes, curve_refs, n)
         curve.start()
         signed = sign * image
@@ -500,7 +509,7 @@
         signed_swapped = swap.field()
         product = signed + signed_swapped
         product_swapped = signed_swapped + there * signed
-        curvature = jnp.sum(curve.finish(), axis=1, keepdims=True)
+        curvature = as_column(curve.finish())
         open_sends.extend([curve, swap])
         step = tiled(rho / curvature)
         residual = residual - step * product
@@ -587,7 +596,7 @@
         dma((ITERS, 2, members)),
         dma((ITERS, 2, members)),
     ]
-    scratch += sum_scratch((2 * loads, order)) + sum_scratch((loads, LANES))
+    scratch += sum_scratch((loads + 1, order)) + sum_scratch((1, LANES))
     scratch += swap_scratch(ITERS + 1, loads, 0)
     scratch += swap_scratch(1, coefs // subs, 8)
     both = pl.pallas_call(

time: 37.2 us -> 35.6 us (0.957)
  Pallas kernels: 36.4 us -> 34.8 us
    pallas_call x1, Pallas kernels: 34.9 us -> 33.4 us  [local(): pl.pallas_call(functools.partial(kernel, sizes), out_shape=jax.ShapeDtype...]
where the time goes in v3:
time: 35.6 us; the launch traced here: 35.4 us
  Pallas kernels  34.8 us (98%)
  between operations  0.64 us (2%)
    pallas_call x1, Pallas kernels, local(): pl.pallas_call(functools.partial(kernel, sizes), out_shape=jax.ShapeDtype...  33.4 us
    pallas_call x1, Pallas kernels, local(): pl.pallas_call(split, out_shape=[jax.ShapeDtypeStruct(rhs.shape, f32)] *...  1.42 us

profile of v3, /device:TPU:0, one launch (start us, length us, event | category | flops | bytes accessed | tf_op | source)
XLA Modules:
  0.0 35.4 jit_solution(14796601520804813192)
XLA Ops:
  0.6 33.4 %shard_map.104.both_ref = f32[2,4,4,384]{3,2,1,0:T(4,128)} custom-call(f32[4,4,384]{2,1,0:T(4,128)} %refs_0_.1, bf16[4,384,384]{2,1,0:T(8,128)(2,1)} %refs_1_.1, s32[4,384]{1,0:T(4,128)} %refs_2_.1, s32[3,4,128]{2,1,0:T(4,128)} %bitcast.1, f32[4,24,384]{2,1,0:T(8,128)} %refs_4_.1, f32[4,8,384]{2,1,0:T(8,128)} %refs_5_.1, s32[4,8]{1,0:T(4,128)} %refs_6_.1, ...), custom_call_target="tpu_custom_call" | custom-call | tf_op jit(solution)/shard_map/pallas_call | solution.py:602
  34.0 1.4 %shard_map.105 = (f32[4,4,384]{2,1,0:T(4,128)}, f32[4,4,384]{2,1,0:T(4,128)}) custom-call(f32[2,4,4,384]{3,2,1,0:T(4,128)} %shard_map.104.both_ref), custom_call_target="tpu_custom_call" | custom-call | tf_op jit(solution)/shard_map/pallas_call | solution.py:610

commit v4 on v3

--- a/solution.py
+++ b/solution.py
@@ -18,6 +18,16 @@
 
 def dot(a, b, dims=NN, precision=HIGHEST):
     return lax.dot_general(a, b, dims, precision=precision, preferred_element_type=jnp.float32)
+
+
+def dot3(a, b, dims=NN):
+    bf16, f32 = jnp.bfloat16, jnp.float32
+    rows = a.shape[0]
+    a_high, b_high = a.astype(bf16).astype(f32), b.astype(bf16)
+    b_low = (b - b_high.astype(f32)).astype(bf16)
+    halves = jnp.concatenate([a_high, a - a_high], axis=0).astype(bf16)
+    out = dot(halves, b_high, dims, None)
+    return out[:rows] + out[rows:] + dot(a_high.astype(bf16), b_low, dims, None)
 
 
 def iota(shape, dim):
@@ -263,9 +273,9 @@
             getattr(piece_copy(n, side, k, step), what)()
 
     def project_start(vector, n):
-        raw = dot(vector, basis_ref[...], NT)
+        raw = dot3(vector, basis_ref[...], NT)
         coef = per_load(jnp.where(diagonal, raw, 0.0))
-        both = dot(coef, weights_ref[...])
+        both = dot3(coef, weights_ref[...])
         tail_refs[0][n, :loads] = both[:, solved:]
         tail_refs[0][n, loads:, :LANES] = as_row(per_load(lanes_added(vector * vector)))
         if order > LANES:
@@ -301,7 +311,7 @@
         summed = tail.finish()
         open_sends.extend([tail, part])
         norm = as_column(summed[loads:, :LANES])
-        corners = dot(summed[:loads], picked_ref[...])
+        corners = dot3(summed[:loads], picked_ref[...])
 
         def amount(base, i):
             return base + corners[:, i * coefs : (i + 1) * coefs]
@@ -309,7 +319,7 @@
         def block_diagonal(x, mask):
             return jnp.where(mask, tiled(x), 0.0)
 
-        fix = dot(block_diagonal(amount(own, 0), diagonal), basis_ref[...])
+        fix = dot3(block_diagonal(amount(own, 0), diagonal), basis_ref[...])
         high = jnp.where(has_high, amount(high, 1), 0.0)
         low = jnp.where(has_low, amount(low, 2), 0.0)
         following = jnp.where(has_next, amount(following, 3), 0.0)
@@ -318,9 +328,9 @@
         cross = jnp.where(odd, following, prev)
         fix_swapped = jnp.concatenate(
             [
-                dot(block_diagonal(high, diagonal), swapped_basis_ref[0]),
-                dot(block_diagonal(low, diagonal), swapped_basis_ref[1]),
-                dot(block_diagonal(cross, crossed), swapped_basis_ref[2]),
+                dot3(block_diagonal(high, diagonal), swapped_basis_ref[0]),
+                dot3(block_diagonal(low, diagonal), swapped_basis_ref[1]),
+                dot3(block_diagonal(cross, crossed), swapped_basis_ref[2]),
             ],
             axis=1,
         )

time: 35.6 us -> 34.6 us (0.972)
  Pallas kernels: 34.8 us -> 33.7 us
    pallas_call x1, Pallas kernels: 33.4 us -> 32.3 us  [local(): pl.pallas_call(functools.partial(kernel, sizes), out_shape=jax.ShapeDtype...]
where the time goes in v4:
time: 34.6 us; the launch traced here: 34.4 us
  Pallas kernels  33.7 us (97%)
  between operations  0.64 us (2%)
    pallas_call x1, Pallas kernels, local(): pl.pallas_call(functools.partial(kernel, sizes), out_shape=jax.ShapeDtype...  32.3 us
    pallas_call x1, Pallas kernels, local(): pl.pallas_call(split, out_shape=[jax.ShapeDtypeStruct(rhs.shape, f32)] *...  1.42 us

profile of v4, /device:TPU:0, one launch (start us, length us, event | category | flops | bytes accessed | tf_op | source)
XLA Modules:
  0.0 34.4 jit_solution(9264370232552842054)
XLA Ops:
  0.6 32.3 %shard_map.104.both_ref = f32[2,4,4,384]{3,2,1,0:T(4,128)} custom-call(f32[4,4,384]{2,1,0:T(4,128)} %refs_0_.1, bf16[4,384,384]{2,1,0:T(8,128)(2,1)} %refs_1_.1, s32[4,384]{1,0:T(4,128)} %refs_2_.1, s32[3,4,128]{2,1,0:T(4,128)} %bitcast.1, f32[4,24,384]{2,1,0:T(8,128)} %refs_4_.1, f32[4,8,384]{2,1,0:T(8,128)} %refs_5_.1, s32[4,8]{1,0:T(4,128)} %refs_6_.1, ...), custom_call_target="tpu_custom_call" | custom-call | tf_op jit(solution)/shard_map/pallas_call | solution.py:612
  33.0 1.4 %shard_map.105 = (f32[4,4,384]{2,1,0:T(4,128)}, f32[4,4,384]{2,1,0:T(4,128)}) custom-call(f32[2,4,4,384]{3,2,1,0:T(4,128)} %shard_map.104.both_ref), custom_call_target="tpu_custom_call" | custom-call | tf_op jit(solution)/shard_map/pallas_call | solution.py:620
